TPU v7x, 32 devices: a whole 2x2x4 slice. The times are simulated.
32 devices in a mesh: clients: 8 (over y, x, core), shard: 4 (over z).
Axes of the slice: x: 2, y: 2, z: 4, core: 2. Of those that a mesh axis runs over, the one named last changes fastest.
Arguments:
- client_deltas: bfloat16 [64, 32, 3584], P(('clients', 'shard')), may hold values from -6 to 6
- variate_deltas: bfloat16 [64, 32, 3584], P(('clients', 'shard')), may hold values from -6 to 6
- params: float32 [32, 3584], P(('clients', 'shard')), may hold values from -1.5 to 1.5
- variate: float32 [32, 3584], P(('clients', 'shard')), may hold values from -1.5 to 1.5
- taking_part: int32 [64], P(('clients', 'shard')), may hold values from 0 to 1, as said below
- counts: int32 [64], P(('clients', 'shard')), may hold values from 32 to 285
Outputs:
- new_params: float32 [32, 3584], P(('clients', 'shard'))
- new_variate: float32 [32, 3584], P(('clients', 'shard'))
- client_params: bfloat16 [32, 3584], replicated
- client_variate: bfloat16 [32, 3584], replicated
Inputs may be any that keep to these rules, and one draw needn't show every extreme that they name: `taking_part`: at least one client takes part.
All inputs are finite; a program needn't handle non-finite values.
Results may differ from a plain program's by a relative error of at most 0.001.
Values may be sent and summed in bfloat16 or wider, within the bound.
A program may use at most 64 MiB of HBM per device.

v0:
```python
import jax
import jax.numpy as jnp
from jax import lax
from jax.sharding import PartitionSpec as P


def weight_rows(taking_part, counts):
    weight = taking_part * counts
    upper_part = weight // 16 * 16
    lower_part = weight - upper_part
    weight_table = jnp.stack([upper_part, lower_part]).astype(jnp.bfloat16)
    chosen = taking_part.astype(jnp.bfloat16)[None, :]
    return (weight_table, chosen, jnp.sum(weight).astype(jnp.float32))


def weigh_blocks(weight_table, chosen, deltas, changes):
    client_count = deltas.shape[0]
    local_rows = deltas.shape[1]
    columns = deltas.shape[2]
    moved_sum = jnp.dot(
        weight_table, deltas.reshape(client_count, -1), preferred_element_type=jnp.float32
    )
    varied = jnp.dot(chosen, changes.reshape(client_count, -1), preferred_element_type=jnp.float32)
    return ((moved_sum[0] + moved_sum[1]).reshape(local_rows, columns), varied)


def body(client_deltas, variate_deltas, params, variate, taking_part, counts):
    all_part, all_counts = (
        lax.all_gather(taking_part, ("clients", "shard"), axis=0, tiled=True),
        lax.all_gather(counts, ("clients", "shard"), axis=0, tiled=True),
    )
    weight_table, chosen, weight_total = weight_rows(all_part, all_counts)
    client_count = all_part.shape[0]
    summed, shifted = weigh_blocks(
        weight_table,
        chosen,
        lax.all_to_all(
            client_deltas, ("clients", "shard"), split_axis=1, concat_axis=0, tiled=True
        ),
        lax.all_to_all(
            variate_deltas, ("clients", "shard"), split_axis=1, concat_axis=0, tiled=True
        ),
    )
    new_params = params + summed / weight_total
    new_variate = variate + shifted / jnp.float32(client_count)
    client_params, client_variate = (
        lax.all_gather(new_params.astype(jnp.bfloat16), ("clients", "shard"), axis=0, tiled=True),
        lax.all_gather(new_variate.astype(jnp.bfloat16), ("clients", "shard"), axis=0, tiled=True),
    )
    return (new_params, new_variate, client_params, client_variate)


def solution(mesh):
    in_specs = (
        P(("clients", "shard"), None, None),
        P(("clients", "shard"), None, None),
        P(("clients", "shard"), None),
        P(("clients", "shard"), None),
        P(("clients", "shard")),
        P(("clients", "shard")),
    )
    out_specs = (P(("clients", "shard"), None), P(("clients", "shard"), None), P(), P())
    return jax.shard_map(body, mesh=mesh, in_specs=in_specs, out_specs=out_specs, check_vma=False)
```

profile of v0, /device:TPU:0, one launch (start us, length us, event | category | flops | bytes accessed | tf_op | source)
XLA Modules:
  0.0 211.8 jit_solution(14549116178163955121)
XLA Ops:
  0.6 2.3 %copy.14 = bf16[2,32,3584]{2,0,1:T(2,128)(2,1)} copy(bf16[2,32,3584]{2,1,0:T(8,128)(2,1)} %param.6) | data formatting | bytes 917504 | tf_op args[0]
  2.9 0.0 copy-start
  2.9 7.3 %all-to-all-start = ((bf16[2,32,3584]{2,0,1:T(2,128)(2,1)}), bf16[2,32,3584]{2,0,1:T(2,128)(2,1)S(1)}, u32[]{:S(2)}, u32[]{:S(2)}) async-start(bf16[2,32,3584]{2,0,1:T(2,128)(2,1)} %copy.14), calls=%async_computation | async-start | bytes 917504 | tf_op jit(solution)/shard_map/all_to_all | solution.py:37
  10.2 0.0 copy-done
  10.2 1.2 copy.15
  11.5 11.7 %all-to-all-done = bf16[2,32,3584]{2,0,1:T(2,128)(2,1)S(1)} async-done(((bf16[2,32,3584]{2,0,1:T(2,128)(2,1)}), bf16[2,32,3584]{2,0,1:T(2,128)(2,1)S(1)}, u32[]{:S(2)}, u32[]{:S(2)}) %all-to-all-start) | async-done | bytes 458784 | tf_op jit(solution)/shard_map/all_to_all | solution.py:37
  23.2 4.1 %all-to-all-start.1 = ((bf16[2,32,3584]{2,0,1:T(2,128)(2,1)}), bf16[2,32,3584]{2,0,1:T(2,128)(2,1)S(1)}, u32[]{:S(2)}, u32[]{:S(2)}) async-start(bf16[2,32,3584]{2,0,1:T(2,128)(2,1)} %copy.15), calls=%async_computation.1 | async-start | bytes 917504 | tf_op jit(solution)/shard_map/all_to_all | solution.py:40
  27.3 0.0 copy-start.3
  27.3 0.6 copy-done.3
  27.9 0.2 dynamic-update-slice
  28.1 0.0 copy-start.4
  28.1 0.7 copy-done.4
  28.8 0.2 dynamic-update-slice.1
  28.9 40.4 %all-reduce.2 = (s32[64]{0:T(128)S(1)}, s32[64]{0:T(128)S(1)}) all-reduce(s32[64]{0:T(128)S(1)} %dynamic-update-slice, s32[64]{0:T(128)S(1)} %dynamic-update-slice.1), channel_id=1, replica_groups=mesh['clients'=8,'shard'=4] {'clients','shard'}, use_global_device_ids=true, to_apply=%add | all-reduce | flops 128 | bytes 1024
  69.4 0.6 convert_bitcast_fusion.2
  70.7 0.2 reshape.22
  70.9 0.0 all-to-all-done.1
  70.9 0.2 reshape.23
  71.1 0.2 convolution_reduce_fusion
  71.3 0.0 copy-start.1
  71.3 0.2 fusion
  71.4 0.5 copy-done.1
  72.0 0.6 convert_bitcast_fusion.1
  72.6 70.0 %all-gather = bf16[32,1,3584]{2,1,0:T(2,128)(2,1)S(1)} all-gather(bf16[1,1,3584]{2,1,0:T(2,128)(2,1)S(1)} %get-tuple-element.8), channel_id=1, replica_groups=mesh['clients'=8,'shard'=4] {'clients','shard'}, dimensions={0}, use_global_device_ids=true | all-gather | bytes 236544 | tf_op jit(solution)/shard_map/all_gather | solution.py:47
  142.6 0.0 copy-start.2
  142.6 0.7 copy.21
  143.3 0.0 copy-done.2
  143.3 0.6 convert_bitcast_fusion
  143.9 67.2 %all-gather.1 = bf16[32,1,3584]{2,1,0:T(2,128)(2,1)S(1)} all-gather(bf16[1,1,3584]{2,1,0:T(2,128)(2,1)S(1)} %get-tuple-element.6), channel_id=1, replica_groups=mesh['clients'=8,'shard'=4] {'clients','shard'}, dimensions={0}, use_global_device_ids=true | all-gather | bytes 236544 | tf_op jit(solution)/shard_map/all_gather | solution.py:48
  211.1 0.7 copy.20
  (4 shorter events, 0.0 us)
Async XLA Ops:
  2.9 7.3 %copy-start = (bf16[2,32,3584]{2,1,0:T(8,128)(2,1)S(1)}, bf16[2,32,3584]{2,1,0:T(8,128)(2,1)}, u32[]{:S(2)}) copy-start(bf16[2,32,3584]{2,1,0:T(8,128)(2,1)} %param.7) | copy-start | bytes 1376260
  2.9 20.3 %all-to-all-start = ((bf16[2,32,3584]{2,0,1:T(2,128)(2,1)}), bf16[2,32,3584]{2,0,1:T(2,128)(2,1)S(1)}, u32[]{:S(2)}, u32[]{:S(2)}) async-start(bf16[2,32,3584]{2,0,1:T(2,128)(2,1)} %copy.14), calls=%async_computation | async-start | bytes 917504 | tf_op jit(solution)/shard_map/all_to_all | solution.py:37
  23.2 47.7 %all-to-all-start.1 = ((bf16[2,32,3584]{2,0,1:T(2,128)(2,1)}), bf16[2,32,3584]{2,0,1:T(2,128)(2,1)S(1)}, u32[]{:S(2)}, u32[]{:S(2)}) async-start(bf16[2,32,3584]{2,0,1:T(2,128)(2,1)} %copy.15), calls=%async_computation.1 | async-start | bytes 917504 | tf_op jit(solution)/shard_map/all_to_all | solution.py:40
  27.3 0.7 copy-start.3
  28.1 0.7 copy-start.4
  71.3 0.7 copy-start.1
  142.6 0.7 copy-start.2
where the time goes:
time: 213 us; the launch traced here: 212 us
  blocking collectives  178 us (84%)
  waiting for transfers between devices  11.7 us (5%)
  starting transfers between devices  11.4 us (5%)
  local copies, waits for them, and re-layouts  7.49 us (4%)
    all_gather x1, blocking collectives, body(): lax.all_gather(new_params.astype(jnp.bfloat16), ('clients', 'shard'), axi...  70 us
    all_gather x1, blocking collectives, body(): lax.all_gather(new_variate.astype(jnp.bfloat16), ('clients', 'shard'), ax...  67.2 us
    unnamed x1, blocking collectives  40.4 us
    all_to_all x1, waiting for transfers between devices, body(): lax.all_to_all(client_deltas, ('clients', 'shard'), split_axis=1, concat_...  11.7 us
    all_to_all x1, starting transfers between devices, body(): lax.all_to_all(client_deltas, ('clients', 'shard'), split_axis=1, concat_...  7.33 us
    unnamed x18, local copies, waits for them, and re-layouts  7.14 us
  transfers between devices with their start and end apart: 2, of which 1 were waited for; matrix products, arithmetic and copies ran while one was open for 1% of the time, Pallas kernels for 0%

commit v1 on v0

v1 whole, which is shorter than its diff:
```python
import functools
import math

import jax
import jax.numpy as jnp
from jax import lax
from jax.experimental import pallas as pl
from jax.experimental.pallas import tpu as pltpu
from jax.sharding import PartitionSpec as P

MESH = pl.DeviceIdType.MESH
LANES = 128
CHUNKS = 2


def split_blocks(blocks, parts):
    parts = min(parts, blocks)
    sizes = [blocks // parts + (1 if i < blocks % parts else 0) for i in range(parts)]
    out, at = [], 0
    for size in sizes:
        out.append((at * LANES, size * LANES))
        at += size
    return out


def kernel(
    cfg,
    cd_ref, vd_ref, p_ref, v_ref, tp_ref, ct_ref,
    np_ref, nv_ref, cp_ref, cv_ref,
    mine, theirs, w_send, w_recv, tot_a, tot_b, tot_c, tot_ra, tot_rb,
    prow, send1, recv1, send2, recv2, fin, land, tp_s, ct_s,
    in_sem, d2d_s, d2d_r, w1s, w1r, w2s, w2r, ps, pr, s1s, s1r, s2s, s2r,
    ags, agr, fws, fwr, os, osr, out_sem,
):
    Q, S, C, R, CB, chunks, clients_total = cfg
    local = cd_ref.shape[0]
    cli = lax.axis_index("clients")
    s = lax.axis_index("shard")
    core = lax.rem(cli, 2)
    q = lax.div(cli, 2)
    other = 1 - core
    B = 2 * C
    sr, sc = lax.div(s, C), lax.rem(s, C)

    def dev(qq, cc, ss):
        return (qq * 2 + cc, ss)

    def rcopy(src, dst, ssem, rsem, device):
        return pltpu.make_async_remote_copy(
            src_ref=src, dst_ref=dst, send_sem=ssem, recv_sem=rsem,
            device_id=device, device_id_type=MESH,
        )

    loads = [
        pltpu.make_async_copy(cd_ref, mine.at[0], in_sem.at[0]),
        pltpu.make_async_copy(vd_ref, mine.at[1], in_sem.at[1]),
        pltpu.make_async_copy(tp_ref, tp_s, in_sem.at[2]),
        pltpu.make_async_copy(ct_ref, ct_s, in_sem.at[3]),
    ]
    for load in loads:
        load.start()

    barrier = pltpu.get_barrier_semaphore()
    for t in range(1, Q * S):
        dq, ds = t // S, t % S
        pl.semaphore_signal(
            barrier, inc=1,
            device_id=dev(lax.rem(q + dq, Q), core, lax.rem(s + ds, S)), device_id_type=MESH,
        )
    for ds in range(S):
        pl.semaphore_signal(
            barrier, inc=1, device_id=dev(q, other, lax.rem(s + ds, S)), device_id_type=MESH
        )

    loads[2].wait()
    loads[3].wait()
    own_w = []
    for i in range(local):
        took = tp_s[i]
        weighed = took * ct_s[i]
        here = jnp.where(core == 0, weighed, took).astype(jnp.float32)
        there = jnp.where(core == 0, took, weighed).astype(jnp.float32)
        own_w.append(here)
        w_send[i] = jnp.full((8, LANES), there, jnp.float32)
    loads[0].wait()
    loads[1].wait()

    pl.semaphore_wait(barrier, Q * S - 1 + S)

    partner = dev(q, other, s)
    w_copy = rcopy(w_send, w_recv, d2d_s.at[0], d2d_r.at[0], partner)
    w_copy.start()
    raw_copy = rcopy(mine.at[other], theirs, d2d_s.at[1], d2d_r.at[1], partner)
    raw_copy.start()

    jj = core * S + s
    j_block, j_in = lax.div(jj, B), lax.rem(jj, B)
    for a, src in enumerate((p_ref, v_ref)):
        for c in range(C):
            to_s = j_block * C + c
            me = jnp.logical_and(core == a, s == to_s)
            piece = src.at[:, pl.ds(c * CB, CB)]

            @pl.when(me)
            def _():
                pltpu.make_async_copy(piece, prow.at[j_in], pr.at[j_in]).start()

            @pl.when(jnp.logical_not(me))
            def _():
                rcopy(piece, prow.at[j_in], ps.at[a, c], pr.at[j_in], dev(q, a, to_s)).start()

    w_copy.wait_recv()
    chip_weight = w_recv[0]
    for i in range(1, local):
        chip_weight = chip_weight + w_recv[i]
    for i in range(local):
        chip_weight = chip_weight + own_w[i]
    tot_a[...] = chip_weight

    raw_copy.wait_recv()
    their_w = [w_recv[i][0:1, 0:1] for i in range(local)]

    def plane_copy(k, d):
        off, width = chunks[k]
        to_q = lax.rem(q + d, Q)
        return rcopy(
            send1.at[to_q, :, pl.ds(C * off, C * width)],
            recv1.at[d - 1, :, pl.ds(C * off, C * width)],
            s1s.at[k, d - 1], s1r.at[k, d - 1], dev(to_q, core, s),
        )

    def tot1_copy(d):
        return rcopy(
            tot_a, tot_ra.at[d - 1], w1s.at[d - 1], w1r.at[d - 1],
            dev(lax.rem(q + d, Q), core, s),
        )

    def tot2_copy(e):
        return rcopy(
            tot_b, tot_rb.at[e - 1], w2s.at[e - 1], w2r.at[e - 1],
            dev(q, core, lax.rem(s + e, S)),
        )

    for k, (off, width) in enumerate(chunks):
        for c in range(C):
            cols = slice(c * CB + off, c * CB + off + width)
            acc = None
            for i in range(local):
                term = mine[core, i, :, cols].astype(jnp.float32) * own_w[i]
                acc = term if acc is None else acc + term
                acc = acc + theirs[i, :, cols].astype(jnp.float32) * their_w[i]
            at = C * off + c * width
            send1[:, :, at:at + width] = acc.reshape(Q, 2 * S, width)
        if k == 0:
            for d in range(1, Q):
                tot1_copy(d).start()
        for d in range(1, Q):
            plane_copy(k, d).start()

    def shard_copy(k, e):
        off, width = chunks[k]
        to_s = lax.rem(s + e, S)
        to_r, to_c = lax.div(to_s, C), lax.rem(to_s, C)
        return rcopy(
            send2.at[to_r, :, pl.ds(pl.multiple_of(C * off + to_c * width, LANES), width)],
            recv2.at[e - 1, :, pl.ds(off, width)],
            s2s.at[k, e - 1], s2r.at[k, e - 1], dev(q, core, to_s),
        )

    for k, (off, width) in enumerate(chunks):
        if k == 0:
            plane_weight = tot_a[...]
            for d in range(1, Q):
                tot1_copy(d).wait_recv()
                plane_weight = plane_weight + tot_ra[d - 1]
            tot_b[...] = plane_weight
        for d in range(1, Q):
            plane_copy(k, d).wait_recv()
        cols = slice(C * off, C * (off + width))
        acc = send1[q, :, cols]
        for d in range(1, Q):
            acc = acc + recv1[d - 1, :, cols]
        send2[:, :, cols] = acc.reshape(R, B, C * width)
        if k == 0:
            for e in range(1, S):
                tot2_copy(e).start()
        for e in range(1, S):
            shard_copy(k, e).start()

    block = q * R + sr

    def piece_cols(c, k):
        off, width = chunks[k]
        return pl.ds(pl.multiple_of(c * CB + off, LANES), width)

    def gather_copy(k, t):
        dq, ds = lax.div(t, S), lax.rem(t, S)
        here = land.at[core, block, :, piece_cols(sc, k)]
        return rcopy(
            here, here, ags.at[k, t], agr.at[k, t],
            dev(lax.rem(q + dq, Q), core, lax.rem(s + ds, S)),
        )

    def source_ref(k, t, a):
        dq, ds = lax.div(t, S), lax.rem(t, S)
        from_q, from_s = lax.rem(q + Q - dq, Q), lax.rem(s + S - ds, S)
        return land.at[
            a, from_q * R + lax.div(from_s, C), :, piece_cols(lax.rem(from_s, C), k)
        ]

    def forward_copy(k, t):
        ref = source_ref(k, t, core)
        return rcopy(ref, ref, fws.at[k, t], fwr.at[k, t], partner)

    def forward_recv(k, t):
        ref = source_ref(k, t, other)
        return rcopy(ref, ref, fws.at[k, t], fwr.at[k, t], partner)

    def row_targets(k):
        off, width = chunks[k]
        for j in range(B):
            row = sr * B + j
            to_core, to_s = lax.div(row, S), lax.rem(row, S)
            me = jnp.logical_and(to_core == core, to_s == s)
            yield j, me, dev(q, to_core, to_s), fin.at[j, :, pl.ds(off, width)]

    for k, (off, width) in enumerate(chunks):
        if k == 0:
            weight_total = tot_b[...]
            for e in range(1, S):
                tot2_copy(e).wait_recv()
                weight_total = weight_total + tot_rb[e - 1]
            tot_c[...] = jnp.where(core == 0, weight_total, jnp.float32(clients_total))
            for j in range(B):
                pltpu.make_async_copy(
                    p_ref.at[:, pl.ds(0, CB)], prow.at[j], pr.at[j]
                ).wait()
        for e in range(1, S):
            shard_copy(k, e).wait_recv()
        acc = send2[sr, :, pl.ds(pl.multiple_of(C * off + sc * width, LANES), width)]
        for e in range(1, S):
            acc = acc + recv2[e - 1, :, off:off + width]
        base = jnp.concatenate([prow[j, :, off:off + width] for j in range(B)], axis=0)
        new = base + acc / tot_c[0:1, 0:1]
        land[core, block, :, piece_cols(sc, k)] = new.astype(jnp.bfloat16)
        for j in range(B):
            fin[j, :, off:off + width] = new[j:j + 1, :]

        @pl.loop(1, Q * S)
        def _(t):
            gather_copy(k, t).start()

        forward_copy(k, 0).start()
        for a, out in enumerate((np_ref, nv_ref)):
            @pl.when(core == a)
            def _():
                for j, me, device, src in row_targets(k):
                    dst = out.at[:, piece_cols(sc, k)]

                    @pl.when(me)
                    def _():
                        pltpu.make_async_copy(src, dst, osr.at[a, sc, k]).start()

                    @pl.when(jnp.logical_not(me))
                    def _():
                        rcopy(src, dst, os.at[j, k], osr.at[a, sc, k], device).start()

    for k in range(len(chunks)):
        @pl.loop(1, Q * S)
        def _(t):
            gather_copy(k, t).wait_recv()
            forward_copy(k, t).start()

    for k in range(len(chunks)):
        @pl.loop(0, Q * S)
        def _(t):
            forward_recv(k, t).wait_recv()

    outs = [
        pltpu.make_async_copy(land.at[0], cp_ref, out_sem.at[0]),
        pltpu.make_async_copy(land.at[1], cv_ref, out_sem.at[1]),
    ]
    for out in outs:
        out.start()

    w_copy.wait_send()
    raw_copy.wait_send()
    for a, src in enumerate((p_ref, v_ref)):
        for c in range(C):
            to_s = j_block * C + c
            me = jnp.logical_and(core == a, s == to_s)

            @pl.when(jnp.logical_not(me))
            def _():
                rcopy(
                    src.at[:, pl.ds(c * CB, CB)], prow.at[j_in], ps.at[a, c], pr.at[j_in],
                    dev(q, a, to_s),
                ).wait_send()
    for d in range(1, Q):
        tot1_copy(d).wait_send()
    for e in range(1, S):
        tot2_copy(e).wait_send()
    for k, (off, width) in enumerate(chunks):
        for d in range(1, Q):
            plane_copy(k, d).wait_send()
        for e in range(1, S):
            shard_copy(k, e).wait_send()

        @pl.loop(1, Q * S)
        def _(t):
            gather_copy(k, t).wait_send()

        @pl.loop(0, Q * S)
        def _(t):
            forward_copy(k, t).wait_send()

        for j, me, device, src in row_targets(k):
            @pl.when(jnp.logical_not(me))
            def _():
                rcopy(
                    src, np_ref.at[:, piece_cols(sc, k)], os.at[j, k], osr.at[0, sc, k], device
                ).wait_send()
        for a, out in enumerate((np_ref, nv_ref)):
            for c in range(C):
                pltpu.make_async_copy(
                    fin.at[0, :, pl.ds(off, width)], out.at[:, piece_cols(c, k)],
                    osr.at[a, c, k],
                ).wait()
    for out in outs:
        out.wait()


def body(sizes, client_deltas, variate_deltas, params, variate, taking_part, counts):
    n_clients, S = sizes
    Q = n_clients // 2
    local, rows, D = client_deltas.shape
    C = math.gcd(S, D // LANES)
    R = S // C
    B = 2 * C
    CB = D // C
    chunks = split_blocks(CB // LANES, CHUNKS)
    K = len(chunks)
    cfg = (Q, S, C, R, CB, chunks, local * n_clients * S)
    f32, bf16 = jnp.float32, jnp.bfloat16
    DMA = pltpu.SemaphoreType.DMA
    any_spec = pl.BlockSpec(memory_space=pl.ANY)
    blocks = rows // B
    new_params, new_variate, cp, cv = pl.pallas_call(
        functools.partial(kernel, cfg),
        out_shape=(
            jax.ShapeDtypeStruct((1, D), f32),
            jax.ShapeDtypeStruct((1, D), f32),
            jax.ShapeDtypeStruct((blocks, B, D), bf16),
            jax.ShapeDtypeStruct((blocks, B, D), bf16),
        ),
        in_specs=[any_spec] * 6,
        out_specs=(any_spec,) * 4,
        scratch_shapes=[
            pltpu.VMEM((2, local, rows, D), bf16),
            pltpu.VMEM((local, rows, D), bf16),
            pltpu.VMEM((local, 8, LANES), f32),
            pltpu.VMEM((local, 8, LANES), f32),
            pltpu.VMEM((8, LANES), f32),
            pltpu.VMEM((8, LANES), f32),
            pltpu.VMEM((8, LANES), f32),
            pltpu.VMEM((Q - 1, 8, LANES), f32),
            pltpu.VMEM((S - 1, 8, LANES), f32),
            pltpu.VMEM((B, 1, CB), f32),
            pltpu.VMEM((Q, 2 * S, D), f32),
            pltpu.VMEM((Q - 1, 2 * S, D), f32),
            pltpu.VMEM((R, B, D), f32),
            pltpu.VMEM((S - 1, B, CB), f32),
            pltpu.VMEM((B, 1, CB), f32),
            pltpu.VMEM((2, blocks, B, D), bf16),
            pltpu.SMEM((local,), jnp.int32),
            pltpu.SMEM((local,), jnp.int32),
            DMA((4,)), DMA((2,)), DMA((2,)),
            DMA((Q - 1,)), DMA((Q - 1,)), DMA((S - 1,)), DMA((S - 1,)),
            DMA((2, C)), DMA((B,)),
            DMA((K, Q - 1)), DMA((K, Q - 1)), DMA((K, S - 1)), DMA((K, S - 1)),
            DMA((K, Q * S)), DMA((K, Q * S)), DMA((K, Q * S)), DMA((K, Q * S)),
            DMA((B, K)), DMA((2, C, K)), DMA((2,)),
        ],
        compiler_params=pltpu.CompilerParams(collective_id=0, has_side_effects=True),
    )(client_deltas, variate_deltas, params, variate, taking_part, counts)
    return new_params, new_variate, cp.reshape(rows, D), cv.reshape(rows, D)


def solution(mesh):
    both = ("clients", "shard")
    in_specs = (
        P(both, None, None),
        P(both, None, None),
        P(both, None),
        P(both, None),
        P(both),
        P(both),
    )
    out_specs = (P(both, None), P(both, None), P(), P())
    sizes = (mesh.shape["clients"], mesh.shape["shard"])
    return jax.shard_map(
        functools.partial(body, sizes),
        mesh=mesh, in_specs=in_specs, out_specs=out_specs, check_vma=False,
    )
```

time: 213 us -> 34.5 us (0.16)
  the two profiles are of different devices: /device:TPU:0 before, /device:TPU:1 now
where the time goes in v1:
time: 34.5 us; the launch traced here: 34.2 us
  Pallas kernels  29.3 us (85%)
  local copies, waits for them, and re-layouts  4.3 us (12%)
  between operations  0.65 us (2%)
    pallas_call x1, Pallas kernels, body(): pl.pallas_call(functools.partial(kernel, cfg), out_shape=(jax.ShapeDtypeS...  29.3 us
    unnamed x8, local copies, waits for them, and re-layouts  4.3 us

profile of v1, /device:TPU:1, one launch (start us, length us, event | category | flops | bytes accessed | tf_op | source)
XLA Modules:
  0.0 34.2 jit_solution(18077084926983668104)
XLA Ops:
  0.6 29.3 %shard_map.93 = (f32[1,3584]{1,0:T(1,128)}, f32[1,3584]{1,0:T(1,128)}, bf16[4,8,3584]{2,1,0:T(8,128)(2,1)}, bf16[4,8,3584]{2,1,0:T(8,128)(2,1)}) custom-call(bf16[2,32,3584]{2,1,0:T(8,128)(2,1)} %cd_ref.1, bf16[2,32,3584]{2,1,0:T(8,128)(2,1)} %vd_ref.1, f32[1,3584]{1,0:T(1,128)} %p_ref.1, f32[1,3584]{1,0:T(1,128)} %v_ref.1, s32[2]{0:T(128)} %tp_ref.1, s32[2]{0:T(128)} %ct_ref.1), custom_call_target="tpu_custom_call" | custom-call | tf_op jit(solution)/shard_map/pallas_call | solution.py:348
  29.9 0.0 copy-start.1
  29.9 1.3 %copy.14 = f32[1,3584]{1,0:T(1,128)} copy(f32[1,3584]{1,0:T(1,128)} %get-tuple-element.16) | data formatting | bytes 28672
  31.2 0.0 copy-done.1
  31.2 0.6 %copy.15 = f32[1,3584]{1,0:T(1,128)} copy(f32[1,3584]{1,0:T(1,128)S(1)} %copy-done.1) | data formatting | bytes 28672
  31.8 0.0 copy-start
  31.8 1.7 %copy.16 = bf16[32,3584]{1,0:T(8,128)(2,1)} copy(bf16[32,3584]{1,0:T(8,128)(2,1)} %bitcast.3) | data formatting | bytes 458752
  33.5 0.0 copy-done
  33.5 0.7 %copy.17 = bf16[32,3584]{1,0:T(8,128)(2,1)} copy(bf16[32,3584]{1,0:T(8,128)(2,1)S(1)} %bitcast.2) | data formatting | bytes 458752
Async XLA Ops:
  29.9 1.3 %copy-start.1 = (f32[1,3584]{1,0:T(1,128)S(1)}, f32[1,3584]{1,0:T(1,128)}, u32[]{:S(2)}) copy-start(f32[1,3584]{1,0:T(1,128)} %get-tuple-element.17) | copy-start | bytes 43012
  31.8 1.7 %copy-start = (bf16[4,8,3584]{2,1,0:T(8,128)(2,1)S(1)}, bf16[4,8,3584]{2,1,0:T(8,128)(2,1)}, u32[]{:S(2)}) copy-start(bf16[4,8,3584]{2,1,0:T(8,128)(2,1)} %get-tuple-element.11) | copy-start | bytes 688132

commit v2 on v1

--- a/solution.py
+++ b/solution.py
@@ -11,6 +11,8 @@
 MESH = pl.DeviceIdType.MESH
 LANES = 128
 CHUNKS = 2
+RELAY = False
+NEAR = True
 
 
 def split_blocks(blocks, parts):
@@ -26,11 +28,11 @@
 def kernel(
     cfg,
     cd_ref, vd_ref, p_ref, v_ref, tp_ref, ct_ref,
-    np_ref, nv_ref, cp_ref, cv_ref,
+    rows, land,
     mine, theirs, w_send, w_recv, tot_a, tot_b, tot_c, tot_ra, tot_rb,
-    prow, send1, recv1, send2, recv2, fin, land, tp_s, ct_s,
+    prow, send1, recv1, send2, recv2, fin, tp_s, ct_s,
     in_sem, d2d_s, d2d_r, w1s, w1r, w2s, w2r, ps, pr, s1s, s1r, s2s, s2r,
-    ags, agr, fws, fwr, os, osr, out_sem,
+    ags, agr, fws, fwr, os, osr,
 ):
     Q, S, C, R, CB, chunks, clients_total = cfg
     local = cd_ref.shape[0]
@@ -61,8 +63,12 @@
         load.start()
 
     barrier = pltpu.get_barrier_semaphore()
+    greeted = S
     for t in range(1, Q * S):
         dq, ds = t // S, t % S
+        if NEAR and dq and ds:
+            continue
+        greeted += 1
         pl.semaphore_signal(
             barrier, inc=1,
             device_id=dev(lax.rem(q + dq, Q), core, lax.rem(s + ds, S)), device_id_type=MESH,
@@ -85,7 +91,7 @@
     loads[0].wait()
     loads[1].wait()
 
-    pl.semaphore_wait(barrier, Q * S - 1 + S)
+    pl.semaphore_wait(barrier, greeted)
 
     partner = dev(q, other, s)
     w_copy = rcopy(w_send, w_recv, d2d_s.at[0], d2d_r.at[0], partner)
@@ -207,6 +213,16 @@
         return land.at[
             a, from_q * R + lax.div(from_s, C), :, piece_cols(lax.rem(from_s, C), k)
         ]
+
+    def relay_copy(k, d, e):
+        ref = source_ref(k, jnp.int32(e), core)
+        return rcopy(
+            ref, ref, ags.at[k, d * S + e], agr.at[k, d * S + e], dev(lax.rem(q + d, Q), core, s)
+        )
+
+    def row_copy(k, j, src, device):
+        dst = rows.at[core, :, piece_cols(sc, k)]
+        return rcopy(src, dst, os.at[j, k], osr.at[core, sc, k], device)
 
     def forward_copy(k, t):
         ref = source_ref(k, t, core)
@@ -246,27 +262,35 @@
         for j in range(B):
             fin[j, :, off:off + width] = new[j:j + 1, :]
 
-        @pl.loop(1, Q * S)
-        def _(t):
-            gather_copy(k, t).start()
+        if RELAY:
+            for e in range(1, S):
+                gather_copy(k, e).start()
+            for d in range(1, Q):
+                relay_copy(k, d, 0).start()
+        else:
+            @pl.loop(1, Q * S)
+            def _(t):
+                gather_copy(k, t).start()
 
         forward_copy(k, 0).start()
-        for a, out in enumerate((np_ref, nv_ref)):
-            @pl.when(core == a)
+        for j, me, device, src in row_targets(k):
+            @pl.when(jnp.logical_not(me))
             def _():
-                for j, me, device, src in row_targets(k):
-                    dst = out.at[:, piece_cols(sc, k)]
-
-                    @pl.when(me)
-                    def _():
-                        pltpu.make_async_copy(src, dst, osr.at[a, sc, k]).start()
-
-                    @pl.when(jnp.logical_not(me))
-                    def _():
-                        rcopy(src, dst, os.at[j, k], osr.at[a, sc, k], device).start()
-
+                row_copy(k, j, src, device).start()
+
+        @pl.when(j_block == sr)
+        def _():
+            rows[core, :, piece_cols(sc, k)] = fin[j_in, :, off:off + width]
+
+    if RELAY:
+        for k in range(len(chunks)):
+            for e in range(1, S):
+                gather_copy(k, e).wait_recv()
+                for d in range(1, Q):
+                    relay_copy(k, d, e).start()
+                forward_copy(k, e).start()
     for k in range(len(chunks)):
-        @pl.loop(1, Q * S)
+        @pl.loop(S if RELAY else 1, Q * S)
         def _(t):
             gather_copy(k, t).wait_recv()
             forward_copy(k, t).start()
@@ -275,13 +299,6 @@
         @pl.loop(0, Q * S)
         def _(t):
             forward_recv(k, t).wait_recv()
-
-    outs = [
-        pltpu.make_async_copy(land.at[0], cp_ref, out_sem.at[0]),
-        pltpu.make_async_copy(land.at[1], cv_ref, out_sem.at[1]),
-    ]
-    for out in outs:
-        out.start()
 
     w_copy.wait_send()
     raw_copy.wait_send()
@@ -306,9 +323,16 @@
         for e in range(1, S):
             shard_copy(k, e).wait_send()
 
-        @pl.loop(1, Q * S)
-        def _(t):
-            gather_copy(k, t).wait_send()
+        if RELAY:
+            for e in range(S):
+                if e:
+                    gather_copy(k, e).wait_send()
+                for d in range(1, Q):
+                    relay_copy(k, d, e).wait_send()
+        else:
+            @pl.loop(1, Q * S)
+            def _(t):
+                gather_copy(k, t).wait_send()
 
         @pl.loop(0, Q * S)
         def _(t):
@@ -317,17 +341,30 @@
         for j, me, device, src in row_targets(k):
             @pl.when(jnp.logical_not(me))
             def _():
-                rcopy(
-                    src, np_ref.at[:, piece_cols(sc, k)], os.at[j, k], osr.at[0, sc, k], device
-                ).wait_send()
-        for a, out in enumerate((np_ref, nv_ref)):
+                row_copy(k, j, src, device).wait_send()
+        for a in range(2):
             for c in range(C):
-                pltpu.make_async_copy(
-                    fin.at[0, :, pl.ds(off, width)], out.at[:, piece_cols(c, k)],
-                    osr.at[a, c, k],
-                ).wait()
-    for out in outs:
-        out.wait()
+                me = jnp.logical_and(core == a, s == j_block * C + c)
+
+                @pl.when(jnp.logical_not(me))
+                def _():
+                    rcopy(
+                        fin.at[0, :, pl.ds(off, width)], rows.at[a, :, piece_cols(c, k)],
+                        os.at[0, k], osr.at[a, c, k], partner,
+                    ).wait_recv()
+
+
+def store_kernel(rows, land, np_ref, nv_ref, cp_ref, cv_ref, sem):
+    copies = [
+        pltpu.make_async_copy(land.at[0], cp_ref, sem.at[0]),
+        pltpu.make_async_copy(land.at[1], cv_ref, sem.at[1]),
+        pltpu.make_async_copy(rows.at[0], np_ref, sem.at[2]),
+        pltpu.make_async_copy(rows.at[1], nv_ref, sem.at[3]),
+    ]
+    for copy in copies:
+        copy.start()
+    for copy in copies:
+        copy.wait()
 
 
 def body(sizes, client_deltas, variate_deltas, params, variate, taking_part, counts):
@@ -345,16 +382,12 @@
     DMA = pltpu.SemaphoreType.DMA
     any_spec = pl.BlockSpec(memory_space=pl.ANY)
     blocks = rows // B
-    new_params, new_variate, cp, cv = pl.pallas_call(
+    vmem_spec = pl.BlockSpec(memory_space=pltpu.VMEM)
+    new_rows, land = pl.pallas_call(
         functools.partial(kernel, cfg),
-        out_shape=(
-            jax.ShapeDtypeStruct((1, D), f32),
-            jax.ShapeDtypeStruct((1, D), f32),
-            jax.ShapeDtypeStruct((blocks, B, D), bf16),
-            jax.ShapeDtypeStruct((blocks, B, D), bf16),
-        ),
+        out_shape=(pltpu.VMEM((2, 1, D), f32), pltpu.VMEM((2, blocks, B, D), bf16)),
         in_specs=[any_spec] * 6,
-        out_specs=(any_spec,) * 4,
+        out_specs=(vmem_spec,) * 2,
         scratch_shapes=[
             pltpu.VMEM((2, local, rows, D), bf16),
             pltpu.VMEM((local, rows, D), bf16),
@@ -371,7 +404,6 @@
             pltpu.VMEM((R, B, D), f32),
             pltpu.VMEM((S - 1, B, CB), f32),
             pltpu.VMEM((B, 1, CB), f32),
-            pltpu.VMEM((2, blocks, B, D), bf16),
             pltpu.SMEM((local,), jnp.int32),
             pltpu.SMEM((local,), jnp.int32),
             DMA((4,)), DMA((2,)), DMA((2,)),
@@ -379,10 +411,22 @@
             DMA((2, C)), DMA((B,)),
             DMA((K, Q - 1)), DMA((K, Q - 1)), DMA((K, S - 1)), DMA((K, S - 1)),
             DMA((K, Q * S)), DMA((K, Q * S)), DMA((K, Q * S)), DMA((K, Q * S)),
-            DMA((B, K)), DMA((2, C, K)), DMA((2,)),
+            DMA((B, K)), DMA((2, C, K)),
         ],
         compiler_params=pltpu.CompilerParams(collective_id=0, has_side_effects=True),
     )(client_deltas, variate_deltas, params, variate, taking_part, counts)
+    new_params, new_variate, cp, cv = pl.pallas_call(
+        store_kernel,
+        out_shape=(
+            jax.ShapeDtypeStruct((1, D), f32),
+            jax.ShapeDtypeStruct((1, D), f32),
+            jax.ShapeDtypeStruct((blocks, B, D), bf16),
+            jax.ShapeDtypeStruct((blocks, B, D), bf16),
+        ),
+        in_specs=[vmem_spec] * 2,
+        out_specs=(any_spec,) * 4,
+        scratch_shapes=[DMA((4,))],
+    )(new_rows, land)
     return new_params, new_variate, cp.reshape(rows, D), cv.reshape(rows, D)
 
 

time: 34.5 us -> 31.5 us (0.913)
  local copies, waits for them, and re-layouts: 4.3 us -> 1.36 us
    unnamed x8 -> x4, local copies, waits for them, and re-layouts: 4.3 us -> 1.36 us
    pallas_call x1 -> x2, Pallas kernels: 29.3 us -> 29.3 us  [the longest x1 27.5 us: body(): pl.pallas_call(functools.partial(kernel, cfg), out_shape=(pltpu.VMEM((2,...]
where the time goes in v2:
time: 31.5 us; the launch traced here: 31.4 us
  Pallas kernels  29.3 us (93%)
  local copies, waits for them, and re-layouts  1.36 us (4%)
  between operations  0.65 us (2%)
    pallas_call x1, Pallas kernels, body(): pl.pallas_call(functools.partial(kernel, cfg), out_shape=(pltpu.VMEM((2,...  27.5 us
    pallas_call x1, Pallas kernels, body(): pl.pallas_call(store_kernel, out_shape=(jax.ShapeDtypeStruct((1, D), f32)...  1.84 us
    unnamed x4, local copies, waits for them, and re-layouts  1.36 us

profile of v2, /device:TPU:1, one launch (start us, length us, event | category | flops | bytes accessed | tf_op | source)
XLA Modules:
  0.0 31.4 jit_solution(5815348088827954635)
XLA Ops:
  0.6 27.5 %shard_map.93 = (f32[2,1,3584]{2,1,0:T(1,128)S(1)}, bf16[2,4,8,3584]{3,2,1,0:T(8,128)(2,1)S(1)}) custom-call(bf16[2,32,3584]{2,1,0:T(8,128)(2,1)} %cd_ref.1, bf16[2,32,3584]{2,1,0:T(8,128)(2,1)} %vd_ref.1, f32[1,3584]{1,0:T(1,128)} %p_ref.1, f32[1,3584]{1,0:T(1,128)} %v_ref.1, s32[2]{0:T(128)} %tp_ref.1, s32[2]{0:T(128)} %ct_ref.1), custom_call_target="tpu_custom_call" | custom-call | tf_op jit(solution)/shard_map/pallas_call | solution.py:386
  28.1 0.0 copy-start
  28.2 0.8 %copy-done = bf16[2,4,8,3584]{3,2,1,0:T(8,128)(2,1)} copy-done((bf16[2,4,8,3584]{3,2,1,0:T(8,128)(2,1)}, bf16[2,4,8,3584]{3,2,1,0:T(8,128)(2,1)S(1)}, u32[]{:S(2)}) %copy-start) | copy-done | bytes 458776
  28.9 0.0 copy-start.1
  28.9 0.6 %copy-done.1 = f32[2,1,3584]{2,1,0:T(1,128)} copy-done((f32[2,1,3584]{2,1,0:T(1,128)}, f32[2,1,3584]{2,1,0:T(1,128)S(1)}, u32[]{:S(2)}) %copy-start.1) | copy-done | bytes 28696
  29.5 1.8 %shard_map.94 = (f32[1,3584]{1,0:T(1,128)}, f32[1,3584]{1,0:T(1,128)}, bf16[4,8,3584]{2,1,0:T(8,128)(2,1)}, bf16[4,8,3584]{2,1,0:T(8,128)(2,1)}) custom-call(f32[2,1,3584]{2,1,0:T(1,128)} %copy-done.1, bf16[2,4,8,3584]{3,2,1,0:T(8,128)(2,1)} %copy-done), custom_call_target="tpu_custom_call" | custom-call | tf_op jit(solution)/shard_map/pallas_call | solution.py:418
Async XLA Ops:
  28.1 0.8 %copy-start = (bf16[2,4,8,3584]{3,2,1,0:T(8,128)(2,1)}, bf16[2,4,8,3584]{3,2,1,0:T(8,128)(2,1)S(1)}, u32[]{:S(2)}) copy-start(bf16[2,4,8,3584]{3,2,1,0:T(8,128)(2,1)S(1)} %get-tuple-element.11.land) | copy-start | bytes 1376260
  28.9 0.6 %copy-start.1 = (f32[2,1,3584]{2,1,0:T(1,128)}, f32[2,1,3584]{2,1,0:T(1,128)S(1)}, u32[]{:S(2)}) copy-start(f32[2,1,3584]{2,1,0:T(1,128)S(1)} %get-tuple-element.10.rows) | copy-start | bytes 86020

commit v3 on v2

--- a/solution.py
+++ b/solution.py
@@ -426,7 +426,10 @@
         in_specs=[vmem_spec] * 2,
         out_specs=(any_spec,) * 4,
         scratch_shapes=[DMA((4,))],
-    )(new_rows, land)
+    )(
+        pltpu.with_memory_space_constraint(new_rows, pltpu.VMEM),
+        pltpu.with_memory_space_constraint(land, pltpu.VMEM),
+    )
     return new_params, new_variate, cp.reshape(rows, D), cv.reshape(rows, D)
 
 

time: 31.5 us -> 29.1 us (0.924)
  local copies, waits for them, and re-layouts: 1.36 us -> 0 us
  Pallas kernels: 29.3 us -> 28.3 us
    unnamed x4 -> x0, local copies, waits for them, and re-layouts: 1.36 us -> none
    pallas_call x1, Pallas kernels: 1.84 us -> 0.8 us  [body(): pl.pallas_call(store_kernel, out_shape=(jax.ShapeDtypeStruct((1, D), f32)...]
where the time goes in v3:
time: 29.1 us; the launch traced here: 28.9 us
  Pallas kernels  28.3 us (97%)
  between operations  0.64 us (2%)
    pallas_call x1, Pallas kernels, body(): pl.pallas_call(functools.partial(kernel, cfg), out_shape=(pltpu.VMEM((2,...  27.5 us
    pallas_call x1, Pallas kernels, body(): pl.pallas_call(store_kernel, out_shape=(jax.ShapeDtypeStruct((1, D), f32)...  0.8 us

profile of v3, /device:TPU:1, one launch (start us, length us, event | category | flops | bytes accessed | tf_op | source)
XLA Modules:
  0.0 28.9 jit_solution(10616534569930331659)
XLA Ops:
  0.6 27.5 %shard_map.93 = (f32[2,1,3584]{2,1,0:T(1,128)S(1)}, bf16[2,4,8,3584]{3,2,1,0:T(8,128)(2,1)S(1)}) custom-call(bf16[2,32,3584]{2,1,0:T(8,128)(2,1)} %cd_ref.1, bf16[2,32,3584]{2,1,0:T(8,128)(2,1)} %vd_ref.1, f32[1,3584]{1,0:T(1,128)} %p_ref.1, f32[1,3584]{1,0:T(1,128)} %v_ref.1, s32[2]{0:T(128)} %tp_ref.1, s32[2]{0:T(128)} %ct_ref.1), custom_call_target="tpu_custom_call" | custom-call | tf_op jit(solution)/shard_map/pallas_call | solution.py:386
  28.1 0.8 %shard_map.94 = (f32[1,3584]{1,0:T(1,128)}, f32[1,3584]{1,0:T(1,128)}, bf16[4,8,3584]{2,1,0:T(8,128)(2,1)}, bf16[4,8,3584]{2,1,0:T(8,128)(2,1)}) custom-call(f32[2,1,3584]{2,1,0:T(1,128)S(1)} %get-tuple-element.10.rows, bf16[2,4,8,3584]{3,2,1,0:T(8,128)(2,1)S(1)} %get-tuple-element.11.land), custom_call_target="tpu_custom_call" | custom-call | tf_op jit(solution)/shard_map/pallas_call | solution.py:418

commit v4 on v3

v4 whole, which is shorter than its diff:
```python
import functools
import math

import jax
import jax.numpy as jnp
from jax import lax
from jax.experimental import pallas as pl
from jax.experimental.pallas import tpu as pltpu
from jax.sharding import PartitionSpec as P

MESH = pl.DeviceIdType.MESH
LANES = 128
SHARES = (3, 4)
RELAYED = ((1, 2, 3), ())
UNROLL = True
FAR_FIRST = True


def split_blocks(blocks):
    out, at, seen = [], 0, 0
    for share in SHARES:
        seen += share
        end = blocks * seen // sum(SHARES)
        if end > at:
            out.append((at * LANES, (end - at) * LANES))
            at = end
    return out


def kernel(
    cfg,
    cd_ref, vd_ref, p_ref, v_ref, tp_ref, ct_ref,
    rows, land,
    mine, pair_send, pair_recv, w_send, w_recv, tot_a, tot_b, tot_c, tot_ra, tot_rb,
    prow, send1, recv1, send2, recv2, fin, tp_s, ct_s,
    in_sem, d2d_s, d2d_r, w1s, w1r, w2s, w2r, ps, pr, s1s, s1r, s2s, s2r,
    ags, agr, fws, fwr, os, osr,
):
    Q, S, C, R, CB, chunks, clients_total = cfg
    local = cd_ref.shape[0]
    cli = lax.axis_index("clients")
    s = lax.axis_index("shard")
    core = lax.rem(cli, 2)
    q = lax.div(cli, 2)
    other = 1 - core
    B = 2 * C
    sr, sc = lax.div(s, C), lax.rem(s, C)
    K = len(chunks)
    far = (lambda n: range(n - 1, 0, -1)) if FAR_FIRST else (lambda n: range(1, n))

    def dev(qq, cc, ss):
        return (qq * 2 + cc, ss)

    def rcopy(src, dst, ssem, rsem, device):
        return pltpu.make_async_remote_copy(
            src_ref=src, dst_ref=dst, send_sem=ssem, recv_sem=rsem,
            device_id=device, device_id_type=MESH,
        )

    loads = [
        pltpu.make_async_copy(cd_ref, mine.at[0], in_sem.at[0]),
        pltpu.make_async_copy(vd_ref, mine.at[1], in_sem.at[1]),
        pltpu.make_async_copy(tp_ref, tp_s, in_sem.at[2]),
        pltpu.make_async_copy(ct_ref, ct_s, in_sem.at[3]),
    ]
    for load in loads:
        load.start()

    barrier = pltpu.get_barrier_semaphore()
    greeted = 0
    for y in range(1, Q):
        greeted += 1
        pl.semaphore_signal(barrier, inc=1, device_id=dev(q ^ y, core, s), device_id_type=MESH)
    for x in range(S):
        for c in (core, other) if x else (other,):
            greeted += 1
            pl.semaphore_signal(barrier, inc=1, device_id=dev(q, c, s ^ x), device_id_type=MESH)

    loads[2].wait()
    loads[3].wait()
    here_w, there_w = [], []
    for i in range(local):
        took = tp_s[i]
        weighed = took * ct_s[i]
        here_w.append(jnp.where(core == 0, weighed, took).astype(jnp.float32))
        there_w.append(jnp.where(core == 0, took, weighed).astype(jnp.float32))
    w_send[...] = jnp.full((8, LANES), sum(there_w), jnp.float32)
    loads[0].wait()
    loads[1].wait()

    def chunk_cols(k):
        off, width = chunks[k]
        return slice(C * off, C * (off + width))

    def weigh(a, weights, cols):
        acc = None
        for i in range(local):
            term = mine[a, i, :, cols].astype(jnp.float32) * weights[i]
            acc = term if acc is None else acc + term
        return acc

    for k in range(len(chunks)):
        cols = chunk_cols(k)
        pair_send[:, cols] = weigh(other, there_w, cols)
        send1[:, :, cols] = weigh(core, here_w, cols).reshape(Q, 2 * S, -1)

    pl.semaphore_wait(barrier, greeted)

    partner = dev(q, other, s)
    w_copy = rcopy(w_send, w_recv, d2d_s.at[K], d2d_r.at[K], partner)
    w_copy.start()

    def pair_copy(k):
        cols = pl.ds(chunk_cols(k).start, C * chunks[k][1])
        return rcopy(
            pair_send.at[:, cols], pair_recv.at[:, cols], d2d_s.at[k], d2d_r.at[k], partner
        )

    for k in range(K):
        pair_copy(k).start()

    def piece_cols(c, k):
        off, width = chunks[k]
        return pl.ds(pl.multiple_of(C * off + c * width, LANES), width)

    jj = core * S + s
    j_block, j_in = lax.div(jj, B), lax.rem(jj, B)
    def base_copies():
        for a, src in enumerate((p_ref, v_ref)):
            for c in range(C):
                to_s = j_block * C + c
                me = jnp.logical_and(core == a, s == to_s)
                for k, (off, width) in enumerate(chunks):
                    piece = src.at[:, pl.ds(C * off + c * width, width)]
                    dst = prow.at[j_in, :, pl.ds(off, width)]
                    yield a, c, k, me, piece, dst, dev(q, a, to_s)

    for a, c, k, me, piece, dst, device in base_copies():
        @pl.when(me)
        def _():
            pltpu.make_async_copy(piece, dst, pr.at[j_in, k]).start()

        @pl.when(jnp.logical_not(me))
        def _():
            rcopy(piece, dst, ps.at[a, c, k], pr.at[j_in, k], device).start()

    w_copy.wait_recv()
    tot_a[...] = w_recv[...] + sum(here_w)

    def plane_copy(k, d):
        off, width = chunks[k]
        to_q = q ^ d
        return rcopy(
            send1.at[to_q, :, pl.ds(C * off, C * width)],
            recv1.at[d - 1, :, pl.ds(C * off, C * width)],
            s1s.at[k, d - 1], s1r.at[k, d - 1], dev(to_q, core, s),
        )

    def tot1_copy(d):
        return rcopy(
            tot_a, tot_ra.at[d - 1], w1s.at[d - 1], w1r.at[d - 1],
            dev(q ^ d, core, s),
        )

    def tot2_copy(e):
        return rcopy(
            tot_b, tot_rb.at[e - 1], w2s.at[e - 1], w2r.at[e - 1],
            dev(q, core, s ^ e),
        )

    for k in range(K):
        cols = chunk_cols(k)
        pair_copy(k).wait_recv()
        send1[:, :, cols] = send1[:, :, cols] + pair_recv[:, cols].reshape(Q, 2 * S, -1)
        if k == 0:
            for d in far(Q):
                tot1_copy(d).start()
        for d in far(Q):
            plane_copy(k, d).start()

    def shard_copy(k, e):
        off, width = chunks[k]
        to_s = s ^ e
        to_r, to_c = lax.div(to_s, C), lax.rem(to_s, C)
        return rcopy(
            send2.at[to_r, :, pl.ds(pl.multiple_of(C * off + to_c * width, LANES), width)],
            recv2.at[e - 1, :, pl.ds(off, width)],
            s2s.at[k, e - 1], s2r.at[k, e - 1], dev(q, core, to_s),
        )

    for k, (off, width) in enumerate(chunks):
        if k == 0:
            plane_weight = tot_a[...]
            for d in range(1, Q):
                tot1_copy(d).wait_recv()
                plane_weight = plane_weight + tot_ra[d - 1]
            tot_b[...] = plane_weight
        for d in range(1, Q):
            plane_copy(k, d).wait_recv()
        cols = slice(C * off, C * (off + width))
        acc = send1[q, :, cols]
        for d in range(1, Q):
            acc = acc + recv1[d - 1, :, cols]
        send2[:, :, cols] = acc.reshape(R, B, C * width)
        if k == 0:
            for e in range(1, S):
                tot2_copy(e).start()
        for e in far(S):
            shard_copy(k, e).start()

    block = q * R + sr

    def gather_copy(k, t):
        here = land.at[core, block, :, piece_cols(sc, k)]
        return rcopy(
            here, here, ags.at[k, t], agr.at[k, t], dev(q ^ (t // S), core, s ^ (t % S))
        )

    def source_ref(k, t, a):
        from_q, from_s = q ^ (t // S), s ^ (t % S)
        return land.at[
            a, from_q * R + lax.div(from_s, C), :, piece_cols(lax.rem(from_s, C), k)
        ]

    def each(first, act):
        if UNROLL and Q * S <= 16:
            for t in order():
                if t >= first:
                    act(t)
        else:
            pl.loop(first, Q * S)(act)

    def relayed(k):
        return [x for x in RELAYED[k] if x < S]

    def relay_copy(k, y, x):
        ref = source_ref(k, x, core)
        t = y * S + x
        return rcopy(ref, ref, ags.at[k, t], agr.at[k, t], dev(q ^ y, core, s))

    def is_direct(k, t):
        return t < S or t % S not in relayed(k)

    def each_direct(k, act):
        if relayed(k):
            for t in order():
                if t and is_direct(k, t):
                    act(t)
        else:
            each(1, act)

    def each_relay(k, act):
        for x in relayed(k):
            for y in range(Q - 1, 0, -1):
                act(y, x)

    def order():
        ts = [y * S + x for x in range(S - 1, -1, -1) for y in range(Q - 1, -1, -1)]
        return ts if FAR_FIRST else ts[::-1]

    def row_copy(k, j, src, device):
        dst = rows.at[core, :, piece_cols(sc, k)]
        return rcopy(src, dst, os.at[j, k], osr.at[core, sc, k], device)

    def forward_copy(k, t):
        ref = source_ref(k, t, core)
        return rcopy(ref, ref, fws.at[k, t], fwr.at[k, t], partner)

    def forward_recv(k, t):
        ref = source_ref(k, t, other)
        return rcopy(ref, ref, fws.at[k, t], fwr.at[k, t], partner)

    def row_targets(k):
        off, width = chunks[k]
        for j in range(B):
            row = sr * B + j
            to_core, to_s = lax.div(row, S), lax.rem(row, S)
            me = jnp.logical_and(to_core == core, to_s == s)
            yield j, me, dev(q, to_core, to_s), fin.at[j, :, pl.ds(off, width)]

    for k, (off, width) in enumerate(chunks):
        if k == 0:
            weight_total = tot_b[...]
            for e in range(1, S):
                tot2_copy(e).wait_recv()
                weight_total = weight_total + tot_rb[e - 1]
            tot_c[...] = jnp.where(core == 0, weight_total, jnp.float32(clients_total))
        for e in range(1, S):
            shard_copy(k, e).wait_recv()
        acc = send2[sr, :, pl.ds(pl.multiple_of(C * off + sc * width, LANES), width)]
        for e in range(1, S):
            acc = acc + recv2[e - 1, :, off:off + width]
        for j in range(B):
            pltpu.make_async_copy(
                p_ref.at[:, pl.ds(0, width)], prow.at[j, :, pl.ds(off, width)], pr.at[j, k]
            ).wait()
        base = jnp.concatenate([prow[j, :, off:off + width] for j in range(B)], axis=0)
        new = base + acc / tot_c[0:1, 0:1]
        land[core, block, :, piece_cols(sc, k)] = new.astype(jnp.bfloat16)
        for j in range(B):
            fin[j, :, off:off + width] = new[j:j + 1, :]

        each_direct(k, lambda t: gather_copy(k, t).start())
        forward_copy(k, 0).start()
        for j, me, device, src in row_targets(k):
            @pl.when(jnp.logical_not(me))
            def _():
                row_copy(k, j, src, device).start()

        @pl.when(j_block == sr)
        def _():
            rows[core, :, piece_cols(sc, k)] = fin[j_in, :, off:off + width]

    for k in range(K):
        for x in relayed(k):
            gather_copy(k, x).wait_recv()
            for y in range(Q - 1, 0, -1):
                relay_copy(k, y, x).start()
            forward_copy(k, x).start()

    w_copy.wait_send()
    for a, c, k, me, piece, dst, device in base_copies():
        @pl.when(jnp.logical_not(me))
        def _():
            rcopy(piece, dst, ps.at[a, c, k], pr.at[j_in, k], device).wait_send()
    for d in range(1, Q):
        tot1_copy(d).wait_send()
    for e in range(1, S):
        tot2_copy(e).wait_send()
    for k in range(K):
        pair_copy(k).wait_send()
        for d in range(1, Q):
            plane_copy(k, d).wait_send()
        for e in range(1, S):
            shard_copy(k, e).wait_send()

    for k in range(K):
        def pass_on(t):
            gather_copy(k, t).wait_recv()
            forward_copy(k, t).start()

        if relayed(k):
            for t in order():
                if t >= S or (t and t not in relayed(k)):
                    pass_on(t)
        else:
            each(1, pass_on)

    for k in range(K):
        each_direct(k, lambda t: gather_copy(k, t).wait_send())
        each_relay(k, lambda y, x: relay_copy(k, y, x).wait_send())
        for j, me, device, src in row_targets(k):
            @pl.when(jnp.logical_not(me))
            def _():
                row_copy(k, j, src, device).wait_send()
    for k in range(K):
        each(0, lambda t: forward_recv(k, t).wait_recv())

    for k, (off, width) in enumerate(chunks):
        each(0, lambda t: forward_copy(k, t).wait_send())
        for a in range(2):
            for c in range(C):
                me = jnp.logical_and(core == a, s == j_block * C + c)

                @pl.when(jnp.logical_not(me))
                def _():
                    rcopy(
                        fin.at[0, :, pl.ds(off, width)], rows.at[a, :, piece_cols(c, k)],
                        os.at[0, k], osr.at[a, c, k], partner,
                    ).wait_recv()


def store_kernel(rows, land, np_ref, nv_ref, cp_ref, cv_ref, sem):
    copies = [
        pltpu.make_async_copy(land.at[0], cp_ref, sem.at[0]),
        pltpu.make_async_copy(land.at[1], cv_ref, sem.at[1]),
        pltpu.make_async_copy(rows.at[0], np_ref, sem.at[2]),
        pltpu.make_async_copy(rows.at[1], nv_ref, sem.at[3]),
    ]
    for copy in copies:
        copy.start()
    for copy in copies:
        copy.wait()


def body(sizes, client_deltas, variate_deltas, params, variate, taking_part, counts):
    n_clients, S = sizes
    Q = n_clients // 2
    local, rows, D = client_deltas.shape
    C = math.gcd(S, D // LANES)
    R = S // C
    B = 2 * C
    CB = D // C
    chunks = split_blocks(CB // LANES)
    K = len(chunks)
    cfg = (Q, S, C, R, CB, chunks, local * n_clients * S)
    f32, bf16 = jnp.float32, jnp.bfloat16
    DMA = pltpu.SemaphoreType.DMA
    any_spec = pl.BlockSpec(memory_space=pl.ANY)
    blocks = rows // B
    vmem_spec = pl.BlockSpec(memory_space=pltpu.VMEM)
    new_rows, land = pl.pallas_call(
        functools.partial(kernel, cfg),
        out_shape=(pltpu.VMEM((2, 1, D), f32), pltpu.VMEM((2, blocks, B, D), bf16)),
        in_specs=[any_spec] * 6,
        out_specs=(vmem_spec,) * 2,
        scratch_shapes=[
            pltpu.VMEM((2, local, rows, D), bf16),
            pltpu.VMEM((rows, D), f32),
            pltpu.VMEM((rows, D), f32),
            pltpu.VMEM((8, LANES), f32),
            pltpu.VMEM((8, LANES), f32),
            pltpu.VMEM((8, LANES), f32),
            pltpu.VMEM((8, LANES), f32),
            pltpu.VMEM((8, LANES), f32),
            pltpu.VMEM((Q - 1, 8, LANES), f32),
            pltpu.VMEM((S - 1, 8, LANES), f32),
            pltpu.VMEM((B, 1, CB), f32),
            pltpu.VMEM((Q, 2 * S, D), f32),
            pltpu.VMEM((Q - 1, 2 * S, D), f32),
            pltpu.VMEM((R, B, D), f32),
            pltpu.VMEM((S - 1, B, CB), f32),
            pltpu.VMEM((B, 1, CB), f32),
            pltpu.SMEM((local,), jnp.int32),
            pltpu.SMEM((local,), jnp.int32),
            DMA((4,)), DMA((K + 1,)), DMA((K + 1,)),
            DMA((Q - 1,)), DMA((Q - 1,)), DMA((S - 1,)), DMA((S - 1,)),
            DMA((2, C, K)), DMA((B, K)),
            DMA((K, Q - 1)), DMA((K, Q - 1)), DMA((K, S - 1)), DMA((K, S - 1)),
            DMA((K, Q * S)), DMA((K, Q * S)), DMA((K, Q * S)), DMA((K, Q * S)),
            DMA((B, K)), DMA((2, C, K)),
        ],
        compiler_params=pltpu.CompilerParams(collective_id=0, has_side_effects=True),
    )(client_deltas, variate_deltas, params, variate, taking_part, counts)
    new_params, new_variate, cp, cv = pl.pallas_call(
        store_kernel,
        out_shape=(
            jax.ShapeDtypeStruct((1, D), f32),
            jax.ShapeDtypeStruct((1, D), f32),
            jax.ShapeDtypeStruct((blocks, B, D), bf16),
            jax.ShapeDtypeStruct((blocks, B, D), bf16),
        ),
        in_specs=[vmem_spec] * 2,
        out_specs=(any_spec,) * 4,
        scratch_shapes=[DMA((4,))],
    )(
        pltpu.with_memory_space_constraint(new_rows, pltpu.VMEM),
        pltpu.with_memory_space_constraint(land, pltpu.VMEM),
    )
    return new_params, new_variate, cp.reshape(rows, D), cv.reshape(rows, D)


def solution(mesh):
    both = ("clients", "shard")
    in_specs = (
        P(both, None, None),
        P(both, None, None),
        P(both, None),
        P(both, None),
        P(both),
        P(both),
    )
    out_specs = (P(both, None), P(both, None), P(), P())
    sizes = (mesh.shape["clients"], mesh.shape["shard"])
    return jax.shard_map(
        functools.partial(body, sizes),
        mesh=mesh, in_specs=in_specs, out_specs=out_specs, check_vma=False,
    )
```

time: 29.1 us -> 27.3 us (0.938)
  Pallas kernels: 28.3 us -> 26.4 us
    pallas_call x1, Pallas kernels: 27.5 us -> 25.6 us  [body(): pl.pallas_call(functools.partial(kernel, cfg), out_shape=(pltpu.VMEM((2,...]
where the time goes in v4:
time: 27.3 us; the launch traced here: 27.1 us
  Pallas kernels  26.4 us (97%)
  between operations  0.64 us (2%)
    pallas_call x1, Pallas kernels, body(): pl.pallas_call(functools.partial(kernel, cfg), out_shape=(pltpu.VMEM((2,...  25.6 us
    pallas_call x1, Pallas kernels, body(): pl.pallas_call(store_kernel, out_shape=(jax.ShapeDtypeStruct((1, D), f32)...  0.8 us

profile of v4, /device:TPU:1, one launch (start us, length us, event | category | flops | bytes accessed | tf_op | source)
XLA Modules:
  0.0 27.1 jit_solution(18008728625326924855)
XLA Ops:
  0.6 25.6 %shard_map.93 = (f32[2,1,3584]{2,1,0:T(1,128)S(1)}, bf16[2,4,8,3584]{3,2,1,0:T(8,128)(2,1)S(1)}) custom-call(bf16[2,32,3584]{2,1,0:T(8,128)(2,1)} %cd_ref.1, bf16[2,32,3584]{2,1,0:T(8,128)(2,1)} %vd_ref.1, f32[1,3584]{1,0:T(1,128)} %p_ref.1, f32[1,3584]{1,0:T(1,128)} %v_ref.1, s32[2]{0:T(128)} %tp_ref.1, s32[2]{0:T(128)} %ct_ref.1), custom_call_target="tpu_custom_call" | custom-call | tf_op jit(solution)/shard_map/pallas_call | solution.py:402
  26.3 0.8 %shard_map.94 = (f32[1,3584]{1,0:T(1,128)}, f32[1,3584]{1,0:T(1,128)}, bf16[4,8,3584]{2,1,0:T(8,128)(2,1)}, bf16[4,8,3584]{2,1,0:T(8,128)(2,1)}) custom-call(f32[2,1,3584]{2,1,0:T(1,128)S(1)} %get-tuple-element.10.rows, bf16[2,4,8,3584]{3,2,1,0:T(8,128)(2,1)S(1)} %get-tuple-element.11.land), custom_call_target="tpu_custom_call" | custom-call | tf_op jit(solution)/shard_map/pallas_call | solution.py:435
